TPU v7x, 32 devices: a whole 2x2x4 slice. The times are simulated.
32 devices in a mesh: batch: 8 (over z, core), vocab: 4 (over y, x).
Axes of the slice: x: 2, y: 2, z: 4, core: 2. Of those that a mesh axis runs over, the one named last changes fastest.
Arguments:
- window_ids: int32 [3, 16, 8], P(None, 'batch'), may hold values from 0 to 16383
- pool_ids: int32 [3, 16, 8], P(None, 'batch'), may hold values from 0 to 16383
- accepted: int32 [2, 16], P(None, 'batch'), may hold values from 1 to 8
- converged: int32 [2, 16], P(None, 'batch'), may hold values 0 or 1
- cache_lens: int32 [16], P('batch'), may hold values from 1 to 128
- table: bfloat16 [16384, 4608], P(('batch', 'vocab')), may hold values from -0.29882812 to 0.29882812
- attn_gain: float32 [4608], replicated, may hold values from 0.25 to 1.75
- post_gain: float32 [4608], replicated, may hold values from 0.25 to 1.75
- final_gain: float32 [4608], replicated, may hold values from 0.25 to 1.75
- w_query: bfloat16 [4608, 1024], P(None, 'vocab'), may hold values from -0.09375 to 0.09375
- w_key: bfloat16 [4608, 512], P(None, 'vocab'), may hold values from -0.09375 to 0.09375
- w_value: bfloat16 [4608, 512], P(None, 'vocab'), may hold values from -0.09375 to 0.09375
- w_out: bfloat16 [1024, 4608], P('vocab'), may hold values from -0.1875 to 0.1875
- cache_keys: bfloat16 [16, 4, 128, 128], P('batch', 'vocab'), may hold values from -6 to 6
- cache_values: bfloat16 [16, 4, 128, 128], P('batch', 'vocab'), may hold values from -6 to 6
Outputs:
- log_total: float32 [3, 16, 8], P(None, 'batch')
- best_logit: float32 [3, 16, 8], P(None, 'batch')
- pool_score: float32 [3, 16, 8], P(None, 'batch')
Inputs may be any that keep to these rules, and one draw needn't show every extreme that they name: `converged`: 1 marks a window at its fixed point, whose tokens are all accepted.
All inputs are finite; a program needn't handle non-finite values. No bound on the sum of `converged` on one device may be relied on, other than what follows from the above.
Results may differ from a plain program's by a relative error of at most 0.00036.
Values may be sent and summed in bfloat16 or wider, within the bound.
No kernel may reach another device: no remote copies, remote signals or barrier semaphores. Data moves between devices by JAX's collectives and lax.ppermute only.
A program may use at most 128 MiB of HBM per device.

v0:
```python
import math
import jax
import jax.numpy as jnp
from jax import lax
from jax.sharding import PartitionSpec as P

epsilon = 1e-06
query_scalar = 144.0
score_cap = 50.0
logit_cap = 30.0


def normalize(values_in, gain):
    return (
        values_in
        * lax.rsqrt(jnp.mean(values_in * values_in, axis=-1, keepdims=True) + epsilon)
        * gain
    )


def rotate(values_in, positions):
    half_size = values_in.shape[-1] // 2
    freqs = 10000.0 ** (-jnp.arange(half_size, dtype=jnp.float32) / half_size)
    angles = positions.astype(jnp.float32)[..., None] * freqs
    cosine = jnp.cos(angles)
    sine = jnp.sin(angles)
    first_half = values_in[..., :half_size]
    second_half = values_in[..., half_size:]
    return jnp.concatenate(
        [first_half * cosine - second_half * sine, second_half * cosine + first_half * sine],
        axis=-1,
    )


def attend(queries, key_rows, value_rows, visible):
    scores = jnp.einsum("bwhgd,bhld->bhgwl", queries, key_rows, preferred_element_type=jnp.float32)
    scores = score_cap * jnp.tanh(scores / score_cap)
    weights = jnp.where(visible[:, None, None], jnp.exp(scores), 0.0)
    weight_sum = jnp.sum(weights, axis=-1, keepdims=True)
    rounded = lax.optimization_barrier(weights.astype(jnp.bfloat16))
    summed = jnp.einsum(
        "bhgwl,bhld->bwhgd", rounded, value_rows, preferred_element_type=jnp.float32
    )
    return (summed / jnp.moveaxis(weight_sum, 3, 1)).astype(jnp.bfloat16)


def per_device(
    window_ids,
    pool_ids,
    accepted,
    converged,
    cache_lens,
    table,
    attn_gain,
    post_gain,
    final_gain,
    w_query,
    w_key,
    w_value,
    w_out,
    cache_keys,
    cache_values,
):
    iter_count, local_batch, width = window_ids.shape
    model_width = table.shape[1]
    vocab_rows = table.shape[0]
    head_size = cache_keys.shape[3]
    kv_local = cache_keys.shape[1]
    cache_slots = cache_keys.shape[2]
    local_rows = local_batch * width
    vocab_devices = lax.axis_size("vocab")
    batch_index = lax.axis_index("batch")
    vocab_index = lax.axis_index("vocab")
    all_windows, all_pools = (
        lax.all_gather(window_ids, "batch", axis=1, tiled=True),
        lax.all_gather(pool_ids, "batch", axis=1, tiled=True),
    )
    total_batch = all_windows.shape[1]
    first_id = (batch_index * vocab_devices + vocab_index) * vocab_rows
    ordered = jnp.transpose(all_windows, (1, 2, 0)) - first_id
    inside = (ordered >= 0) & (ordered < vocab_rows)
    looked_up = jnp.take(table, jnp.clip(ordered, 0, vocab_rows - 1), axis=0)
    lookup_terms = jnp.where(inside[..., None], looked_up.astype(jnp.float32), 0.0)
    column_rows = lax.psum_scatter(
        lookup_terms.astype(jnp.bfloat16), "batch", scatter_dimension=0, tiled=True
    )
    embedded_all = lax.psum(column_rows, "vocab").astype(jnp.float32)
    taken = jnp.where(converged == 1, width, accepted)
    offset = cache_lens
    slots = jnp.arange(width, dtype=jnp.int32)
    cache_visible = (
        jnp.arange(cache_slots, dtype=jnp.int32)[None, None, :] < cache_lens[:, None, None]
    )
    own_visible = slots[None, None, :] <= slots[None, :, None]
    key_list = [cache_keys]
    value_list = [cache_values]
    mask_list = [jnp.broadcast_to(cache_visible, (local_batch, width, cache_slots))]
    vocab_iota = jnp.arange(vocab_rows, dtype=jnp.int32)
    totals_out = []
    best_out = []
    score_out = []
    for step in range(iter_count):
        embedded = embedded_all[:, :, step] * math.sqrt(model_width)
        normed = (
            normalize(embedded, attn_gain).astype(jnp.bfloat16).reshape(local_rows, model_width)
        )
        positions = (offset[:, None] + slots[None, :])[:, :, None]
        queries = jnp.dot(normed, w_query, preferred_element_type=jnp.float32).reshape(
            local_batch, width, 2 * kv_local, head_size
        )
        queries = (
            (rotate(queries, positions) / math.sqrt(query_scalar))
            .astype(jnp.bfloat16)
            .reshape(local_batch, width, kv_local, 2, head_size)
        )
        keys_now = jnp.dot(normed, w_key, preferred_element_type=jnp.float32).reshape(
            local_batch, width, kv_local, head_size
        )
        keys_now = rotate(keys_now, positions).astype(jnp.bfloat16).transpose(0, 2, 1, 3)
        values_now = jnp.dot(normed, w_value, preferred_element_type=jnp.float32).reshape(
            local_batch, width, kv_local, head_size
        )
        values_now = values_now.astype(jnp.bfloat16).transpose(0, 2, 1, 3)
        all_keys = jnp.concatenate(key_list + [keys_now], axis=2)
        all_values = jnp.concatenate(value_list + [values_now], axis=2)
        visible = jnp.concatenate(
            mask_list + [jnp.broadcast_to(own_visible, (local_batch, width, width))], axis=2
        )
        attended = attend(queries, all_keys, all_values, visible).reshape(
            local_rows, 2 * kv_local * head_size
        )
        branch = jnp.dot(attended, w_out, preferred_element_type=jnp.float32)
        residual = embedded.reshape(local_rows, model_width)
        whole_branch = lax.psum(branch, "vocab")
        hidden = residual + normalize(whole_branch, post_gain)
        final_rows = normalize(hidden, final_gain).astype(jnp.bfloat16)
        pool_local = all_pools[step].reshape(total_batch * width) - first_id
        raw_logits = lax.dot_general(
            lax.all_gather(final_rows, "batch", axis=0, tiled=True),
            table,
            (((1,), (1,)), ((), ())),
            preferred_element_type=jnp.float32,
        )
        logits = logit_cap * jnp.tanh(raw_logits / logit_cap)
        exp_sums = jnp.sum(jnp.exp(logits), axis=-1)
        largest = jnp.max(logits, axis=-1)
        chosen = jnp.sum(
            jnp.where(vocab_iota[None, :] == pool_local[:, None], logits, 0.0), axis=-1
        )
        own_start = batch_index * local_rows
        sums_column, picks_column = (
            lax.psum_scatter(exp_sums, "batch", scatter_dimension=0, tiled=True),
            lax.psum_scatter(chosen, "batch", scatter_dimension=0, tiled=True),
        )
        sums_own, picks_own = lax.psum((sums_column, picks_column), "vocab")
        tops_joint = lax.pmax(largest, ("batch", "vocab"))
        tops_own = lax.dynamic_slice_in_dim(tops_joint, own_start, local_rows)
        log_sum = jnp.log(sums_own)
        totals_out.append(log_sum.reshape(local_batch, width))
        best_out.append(tops_own.reshape(local_batch, width))
        score_out.append((picks_own - log_sum).reshape(local_batch, width))
        if step + 1 < iter_count:
            key_list.append(keys_now)
            value_list.append(values_now)
            mask_list.append(
                jnp.broadcast_to(
                    slots[None, None, :] < taken[step][:, None, None], (local_batch, width, width)
                )
            )
            offset = offset + taken[step]
    return (jnp.stack(totals_out), jnp.stack(best_out), jnp.stack(score_out))


def solution(mesh):
    return jax.shard_map(
        per_device,
        mesh=mesh,
        in_specs=(
            P(None, "batch", None),
            P(None, "batch", None),
            P(None, "batch"),
            P(None, "batch"),
            P("batch"),
            P(("batch", "vocab"), None),
            P(),
            P(),
            P(),
            P(None, "vocab"),
            P(None, "vocab"),
            P(None, "vocab"),
            P("vocab", None),
            P("batch", "vocab", None, None),
            P("batch", "vocab", None, None),
        ),
        out_specs=(P(None, "batch", None), P(None, "batch", None), P(None, "batch", None)),
        check_vma=False,
    )
```

profile of v0, /device:TPU:10, one launch (start us, length us, event | category | flops | bytes accessed | tf_op | source)
XLA Modules:
  0.0 360.0 jit_solution(6029630634133774123)
XLA Ops:
  7.2 0.8 copy.76
  8.1 14.3 %all_gather.15 = s32[3,16,8]{2,0,1:T(4,128)S(1)} all-gather(s32[3,2,8]{2,0,1:T(4,128)S(1)} %copy.76), channel_id=1, replica_groups=mesh['batch'=8,'vocab'=4] {'batch'}, dimensions={1}, use_global_device_ids=true | all-gather | bytes 1728 | tf_op jit(solution)/shard_map/all_gather | solution.py:75
  22.8 12.2 %gather_fusion = bf16[384,4608]{1,0:T(8,128)(2,1)} fusion(bf16[512,4608]{1,0:T(8,128)(2,1)} %param.20, s32[1024]{0:T(1024)S(1)} %pad_clamp_fusion), kind=kCustom, calls=%fused_computation | custom fusion | bytes 7079424 | tf_op jit(solution)/shard_map/jit(_take)/gather | solution.py:82
  35.0 7.3 %reshape.718 = bf16[16,8,3,4608]{3,2,1,0:T(4,128)(2,1)} reshape(bf16[384,4608]{1,0:T(8,128)(2,1)} %gather_fusion) | data formatting | bytes 7077888 | tf_op jit(solution)/shard_map/jit(_take)/gather | solution.py:82
  42.4 6.3 %select_convert_fusion = bf16[16,8,3,4608]{3,1,2,0:T(8,128)(2,1)} fusion(bf16[16,8,3,4608]{3,2,1,0:T(4,128)(2,1)} %reshape.718, pred[16,8,3]{1,2,0:T(4,128)(4,1)S(1)} %copy.79, pred[16,8,3]{1,2,0:T(4,128)(4,1)S(1)} %copy.78), kind=kLoop, calls=%fused_computation.1 | loop fusion | flops 7077888 | bytes 7078656 | tf_op jit(solution)/shard_map/convert_element_type | solution.py:85
  48.8 4.3 %copy.102 = bf16[256,4608]{1,0:T(8,128)(2,1)} copy(bf16[256,4608]{0,1:T(8,128)(2,1)} %bitcast.314) | data formatting | bytes 4718592 | tf_op jit(solution)/shard_map/dot_general | solution.py:108
  53.7 36.1 %reduce-scatter.2.cloned.1.call-done = bf16[2,8,3,4608]{3,1,2,0:T(8,128)(2,1)} async-done(((bf16[16,8,3,4608]{3,1,2,0:T(8,128)(2,1)}), bf16[2,8,3,4608]{3,1,2,0:T(8,128)(2,1)}) %reduce-scatter.2.cloned.1.call-update) | async-done | bytes 442384 | tf_op jit(solution)/shard_map/reduce_scatter | solution.py:84
  89.8 1.8 copy.82
  92.1 47.6 %all-reduce.13.cloned.1.call-done = bf16[2,8,3,4608]{3,1,0,2:T(8,128)(2,1)} async-done(((bf16[2,8,3,4608]{3,1,0,2:T(8,128)(2,1)}), bf16[2,8,3,4608]{3,1,0,2:T(8,128)(2,1)}) %all-reduce.13.cloned.1.call-update) | async-done | bytes 442384 | tf_op jit(solution)/shard_map/psum | solution.py:87
  139.7 1.2 convert_element_type.164
  141.1 1.6 fusion.45
  142.7 1.7 fusion.48
  147.1 0.7 fusion.89
  149.9 1.2 fusion.71
  151.1 1.2 fusion.70
  152.4 1.2 fusion.69
  153.7 50.5 %all-reduce.15.cloned.1.call-done = (f32[16,4608]{1,0:T(8,128)}, f32[16,4608]{1,0:T(8,128)}, f32[16,4608]{1,0:T(8,128)}) async-done(((f32[16,4608]{1,0:T(8,128)}, f32[16,4608]{1,0:T(8,128)}, f32[16,4608]{1,0:T(8,128)}), (f32[16,4608]{1,0:T(8,128)}, f32[16,4608]{1,0:T(8,128)}, f32[16,4608]{1,0:T(8,128)})) %all-reduce.15.cloned.1.call-update) | async-done | bytes 884752 | tf_op jit(solution)/shard_map/psum | solution.py:134
  204.2 1.2 multiply_reduce_fusion.1
  205.4 1.1 multiply_reduce_fusion.3
  206.5 1.1 multiply_reduce_fusion.5
  207.7 1.5 multiply_reduce_fusion.4
  209.3 1.0 multiply_convert_fusion.4
  211.5 14.2 %all_gather.19 = s32[3,16,8]{2,0,1:T(4,128)S(1)} all-gather(s32[3,2,8]{2,0,1:T(4,128)S(1)} %copy.92), channel_id=1, replica_groups=mesh['batch'=8,'vocab'=4] {'batch'}, dimensions={1}, use_global_device_ids=true | all-gather | bytes 1728 | tf_op jit(solution)/shard_map/all_gather | solution.py:76
  227.3 5.9 %all-gather.4.cloned.1.call-done = bf16[128,4608]{1,0:T(8,128)(2,1)} async-done(((bf16[16,4608]{1,0:T(8,128)(2,1)}), bf16[128,4608]{1,0:T(8,128)(2,1)}) %all-gather.4.cloned.1.call-update) | async-done | bytes 1179664 | tf_op jit(solution)/shard_map/all_gather | solution.py:139
  233.2 4.5 %select_reduce_fusion.2 = (f32[128]{0:T(128)S(1)}, f32[128]{0:T(128)S(1)}, f32[128]{0:T(128)S(1)}) fusion(s32[128]{0:T(128)S(1)} %sub.79, bf16[128,4608]{1,0:T(8,128)(2,1)} %all-gather.4.cloned.1.call-done, bf16[512,4608]{1,0:T(8,128)(2,1)} %param.20), kind=kOutput, calls=%fused_computation.103 | convolution fusion | flops 604438144 | bytes 5900288 | tf_op jit(solution)/shard_map/dot_general | solution.py:138
  237.7 19.4 %all-gather.6.cloned.1.call-done = bf16[128,4608]{1,0:T(8,128)(2,1)} async-done(((bf16[16,4608]{1,0:T(8,128)(2,1)}), bf16[128,4608]{1,0:T(8,128)(2,1)}) %all-gather.6.cloned.1.call-update) | async-done | bytes 1179664 | tf_op jit(solution)/shard_map/all_gather | solution.py:139
  257.1 4.5 %select_reduce_fusion.1 = (f32[128]{0:T(128)S(1)}, f32[128]{0:T(128)S(1)}, f32[128]{0:T(128)S(1)}) fusion(s32[128]{0:T(128)S(1)} %sub.82, bf16[128,4608]{1,0:T(8,128)(2,1)} %all-gather.6.cloned.1.call-done, bf16[512,4608]{1,0:T(8,128)(2,1)} %param.20), kind=kOutput, calls=%fused_computation.101 | convolution fusion | flops 604438144 | bytes 5900288 | tf_op jit(solution)/shard_map/dot_general | solution.py:138
  261.6 19.5 %all-gather.8.cloned.1.call-done = bf16[128,4608]{1,0:T(8,128)(2,1)} async-done(((bf16[16,4608]{1,0:T(8,128)(2,1)}), bf16[128,4608]{1,0:T(8,128)(2,1)}) %all-gather.8.cloned.1.call-update) | async-done | bytes 1179664 | tf_op jit(solution)/shard_map/all_gather | solution.py:139
  281.0 4.5 %select_reduce_fusion = (f32[128]{0:T(128)S(1)}, f32[128]{0:T(128)S(1)}, f32[128]{0:T(128)S(1)}) fusion(s32[128]{0:T(128)S(1)} %sub.85, bf16[128,4608]{1,0:T(8,128)(2,1)} %all-gather.8.cloned.1.call-done, bf16[512,4608]{1,0:T(8,128)(2,1)} %param.20), kind=kOutput, calls=%fused_computation.99 | convolution fusion | flops 604438144 | bytes 5900288 | tf_op jit(solution)/shard_map/dot_general | solution.py:138
  285.5 12.1 %all-reduce.7 = (f32[128]{0:T(128)S(1)}, f32[128]{0:T(128)S(1)}, f32[128]{0:T(128)S(1)}, f32[128]{0:T(128)S(1)}, f32[128]{0:T(128)S(1)}, /*index=5*/f32[128]{0:T(128)S(1)}) all-reduce(f32[128]{0:T(128)S(1)} %get-tuple-element.17, f32[128]{0:T(128)S(1)} %get-tuple-element.14, ...), channel_id=5, replica_groups=mesh['batch'=8,'vocab'=4] {'batch'}, use_global_device_ids=true, to_apply=%region_24.25.clone | all-reduce | flops 768 | bytes 6144
  298.1 8.0 %all-reduce.8 = (f32[16]{0:T(128)S(1)}, f32[16]{0:T(128)S(1)}, f32[16]{0:T(128)S(1)}, f32[16]{0:T(128)S(1)}, f32[16]{0:T(128)S(1)}, /*index=5*/f32[16]{0:T(128)S(1)}) all-reduce(f32[16]{0:T(128)S(1)} %dynamic-slice.5, f32[16]{0:T(128)S(1)} %dynamic-slice.3, f32[16]{0:T(128)S(1)} %dynamic-slice.1, ...), channel_id=1, replica_groups=mesh['batch'=8,'vocab'=4] {'vocab'}, use_global_device_ids=true, to_apply=%region_25.26 | all-reduce | flops 96 | bytes 768 | tf_op jit(solution)/shard_map/psum | solution.py:155
  306.4 44.3 %all-reduce.6 = (f32[128]{0:T(128)S(1)}, f32[128]{0:T(128)S(1)}, f32[128]{0:T(128)S(1)}) all-reduce(f32[128]{0:T(128)S(1)} %get-tuple-element.16, f32[128]{0:T(128)S(1)} %get-tuple-element.13, f32[128]{0:T(128)S(1)} %get-tuple-element.10), channel_id=1, replica_groups=mesh['batch'=8,'vocab'=4] {'batch','vocab'}, use_global_device_ids=true, to_apply=%region_31.32 | all-reduce | flops 384 | bytes 3072 | tf_op jit(solution)/shard_map/pmax | solution.py:156
  (123 shorter events, 12.0 us)
Async XLA Ops:
  7.2 142.7 %copy-start = (bf16[256,4608]{1,0:T(8,128)(2,1)S(1)}, bf16[256,4608]{1,0:T(8,128)(2,1)}, u32[]{:S(2)}) copy-start(bf16[256,4608]{1,0:T(8,128)(2,1)} %param.27) | copy-start | bytes 7077892
  7.2 82.6 %reduce-scatter.2.cloned.1.call-start = ((), (), s32[]{:S(2)}) async-start(), calls=%async_computation.1 | async-start | bytes 3981312 | tf_op jit(solution)/shard_map/reduce_scatter | solution.py:84
  48.7 90.9 %all-reduce.13.cloned.1.call-start = ((), (), s32[]{:S(2)}) async-start(), calls=%async_computation.2 | async-start | bytes 884736 | tf_op jit(solution)/shard_map/psum | solution.py:87
  48.8 4.4 %copy-start.14 = (s32[2]{0:T(128)S(1)}, s32[2]{0:T(128)}, u32[]{:S(2)}) copy-start(s32[2]{0:T(128)} %param.19) | copy-start | bytes 28
  48.8 4.5 %copy-start.12 = (s32[2,2]{1,0:T(2,128)S(1)}, s32[2,2]{1,0:T(2,128)}, u32[]{:S(2)}) copy-start(s32[2,2]{1,0:T(2,128)} %param.17) | copy-start | bytes 52
  48.8 4.5 %copy-start.13 = (s32[2,2]{1,0:T(2,128)S(1)}, s32[2,2]{1,0:T(2,128)}, u32[]{:S(2)}) copy-start(s32[2,2]{1,0:T(2,128)} %param.18) | copy-start | bytes 52
  53.2 87.9 %copy-start.4 = (f32[4608]{0:T(1024)S(1)}, f32[4608]{0:T(1024)}, u32[]{:S(2)}) copy-start(f32[4608]{0:T(1024)} %param.21) | copy-start | bytes 55300
  91.6 112.6 %all-reduce.15.cloned.1.call-start = ((), (), s32[]{:S(2)}) async-start(), calls=%async_computation.6 | async-start | bytes 1769472 | tf_op jit(solution)/shard_map/psum | solution.py:134
  139.7 4.7 %copy-start.3 = (bf16[4608,128]{1,0:T(8,128)(2,1)S(1)}, bf16[4608,128]{1,0:T(8,128)(2,1)}, u32[]{:S(2)}) copy-start(bf16[4608,128]{1,0:T(8,128)(2,1)} %param.26) | copy-start | bytes 3538948
  142.6 2.4 copy-start.2
  144.7 1.7 copy-start.1
  147.1 1.7 copy-start.15
  147.8 2.1 copy-start.8
  152.4 55.3 %copy-start.9 = (f32[4608]{0:T(1024)S(1)}, f32[4608]{0:T(1024)}, u32[]{:S(2)}) copy-start(f32[4608]{0:T(1024)} %param.22) | copy-start | bytes 55300
  153.6 55.6 %copy-start.10 = (f32[4608]{0:T(1024)S(1)}, f32[4608]{0:T(1024)}, u32[]{:S(2)}) copy-start(f32[4608]{0:T(1024)} %param.23) | copy-start | bytes 55300
  153.6 79.6 %all-gather.4.cloned.1.call-start = ((), (), s32[]{:S(2)}) async-start(), calls=%async_computation.3 | async-start | bytes 1327104 | tf_op jit(solution)/shard_map/all_gather | solution.py:139
  204.2 5.1 %copy-start.5 = (f32[16,4608]{1,0:T(8,128)S(1)}, f32[16,4608]{1,0:T(8,128)}, u32[]{:S(2)}) copy-start(f32[16,4608]{1,0:T(8,128)} %get-tuple-element.36) | copy-start | bytes 884740
  204.2 5.1 %copy-start.6 = (f32[16,4608]{1,0:T(8,128)S(1)}, f32[16,4608]{1,0:T(8,128)}, u32[]{:S(2)}) copy-start(f32[16,4608]{1,0:T(8,128)} %get-tuple-element.37) | copy-start | bytes 884740
  204.2 5.1 %copy-start.7 = (f32[16,4608]{1,0:T(8,128)S(1)}, f32[16,4608]{1,0:T(8,128)}, u32[]{:S(2)}) copy-start(f32[16,4608]{1,0:T(8,128)} %get-tuple-element.38) | copy-start | bytes 884740
  206.5 4.9 %copy-start.11 = (s32[3,2,8]{2,1,0:T(2,128)S(1)}, s32[3,2,8]{2,1,0:T(2,128)}, u32[]{:S(2)}) copy-start(s32[3,2,8]{2,1,0:T(2,128)} %param.16) | copy-start | bytes 580
  207.6 18.4 %copy-start.16 = (u32[32]{0:T(128)S(1)}, u32[32]{0:T(128)}, u32[]{:S(2)}) copy-start(u32[32]{0:T(128)} %constant.94) | copy-start | bytes 388
  210.3 46.8 %all-gather.6.cloned.1.call-start = ((), (), s32[]{:S(2)}) async-start(), calls=%async_computation.4 | async-start | bytes 1327104 | tf_op jit(solution)/shard_map/all_gather | solution.py:139
  210.9 70.2 %all-gather.8.cloned.1.call-start = ((), (), s32[]{:S(2)}) async-start(), calls=%async_computation.5 | async-start | bytes 1327104 | tf_op jit(solution)/shard_map/all_gather | solution.py:139
Sparse Core Ops, SparseCore 0:
  48.9 40.8 reduce-scatter.1
  92.8 46.8 all-reduce.12
  153.7 50.3 all-reduce.14
  210.4 22.7 all-gather.3
  234.7 22.3 all-gather.5
  258.6 22.4 all-gather.7
where the time goes:
time: 361 us; the launch traced here: 360 us
  waiting for transfers between devices  180 us (50%)
  blocking collectives  92.9 us (26%)
  local copies, waits for them, and re-layouts  30 us (8%)
  matrix products  24.9 us (7%)
  other arithmetic  16.6 us (5%)
  between operations  15.1 us (4%)
    psum x1, waiting for transfers between devices, per_device(): whole_branch = lax.psum(branch, 'vocab')  50.5 us
    psum x1, waiting for transfers between devices, per_device(): embedded_all = lax.psum(column_rows, 'vocab').astype(jnp.float32)  47.6 us
    all_gather x3, waiting for transfers between devices, per_device(): lax.all_gather(final_rows, 'batch', axis=0, tiled=True)  44.7 us
    pmax x1, blocking collectives, per_device(): tops_joint = lax.pmax(largest, ('batch', 'vocab'))  44.3 us
    reduce_scatter x1, waiting for transfers between devices, per_device(): lax.psum_scatter(lookup_terms.astype(jnp.bfloat16), 'batch', scatter_dime...  36.1 us
    gather x2, local copies, waits for them, and re-layouts, per_device(): looked_up = jnp.take(table, jnp.clip(ordered, 0, vocab_rows - 1), axis=0)  19.4 us
    all_gather x1, blocking collectives, per_device(): lax.all_gather(window_ids, 'batch', axis=1, tiled=True)  14.3 us
    all_gather x1, blocking collectives, per_device(): lax.all_gather(pool_ids, 'batch', axis=1, tiled=True)  14.2 us
  transfers between devices with their start and end apart: 6, of which 6 were waited for; matrix products, arithmetic and copies ran while one was open for 4% of the time, Pallas kernels for 0%

commit v1 on v0

--- a/solution.py
+++ b/solution.py
@@ -136,7 +136,10 @@
         final_rows = normalize(hidden, final_gain).astype(jnp.bfloat16)
         pool_local = all_pools[step].reshape(total_batch * width) - first_id
         raw_logits = lax.dot_general(
-            lax.all_gather(final_rows, "batch", axis=0, tiled=True),
+            jnp.concatenate(
+                lax.all_to_all(jnp.stack([final_rows] * lax.axis_size("batch")), "batch", 0, 0),
+                axis=0,
+            ),
             table,
             (((1,), (1,)), ((), ())),
             preferred_element_type=jnp.float32,

time: 361 us -> 406 us (1.12)
  blocking collectives: 92.9 us -> 178 us
  waiting for transfers between devices: 180 us -> 134 us
  starting transfers between devices: 0.42 us -> 6.25 us
    all_to_all x0 -> x2, blocking collectives: none -> 65.1 us  [per_device(): lax.all_to_all(jnp.stack([final_rows] * lax.axis_size('batch')), 'batch',...]
    all_gather x3 -> x0, waiting for transfers between devices: 44.7 us -> none  [per_device(): lax.all_gather(final_rows, 'batch', axis=0, tiled=True)]
    all_gather x1, blocking collectives: 14.2 us -> 34.3 us  [per_device(): lax.all_gather(pool_ids, 'batch', axis=1, tiled=True)]
    all_to_all x0 -> x1, starting transfers between devices: none -> 5.95 us  [per_device(): lax.all_to_all(jnp.stack([final_rows] * lax.axis_size('batch')), 'batch',...]
  transfers between devices with their start and end apart: 6 -> 4, of which waited for: 6 -> 3; matrix products, arithmetic and copies ran while one was open for 4% -> 4% of each run, Pallas kernels for 0% -> 0%
where the time goes in v1:
time: 406 us; the launch traced here: 405 us
  blocking collectives  178 us (44%)
  waiting for transfers between devices  134 us (33%)
  local copies, waits for them, and re-layouts  31.3 us (8%)
  matrix products  24.6 us (6%)
  other arithmetic  15.9 us (4%)
  between operations  14.7 us (4%)
  starting transfers between devices  6.25 us (2%)
    all_to_all x2, blocking collectives, per_device(): lax.all_to_all(jnp.stack([final_rows] * lax.axis_size('batch')), 'batch',...  65.1 us
    psum x1, waiting for transfers between devices, per_device(): whole_branch = lax.psum(branch, 'vocab')  50.6 us
    psum x1, waiting for transfers between devices, per_device(): embedded_all = lax.psum(column_rows, 'vocab').astype(jnp.float32)  47.6 us
    pmax x1, blocking collectives, per_device(): tops_joint = lax.pmax(largest, ('batch', 'vocab'))  43.5 us
    reduce_scatter x1, waiting for transfers between devices, per_device(): lax.psum_scatter(lookup_terms.astype(jnp.bfloat16), 'batch', scatter_dime...  36.1 us
    all_gather x1, blocking collectives, per_device(): lax.all_gather(pool_ids, 'batch', axis=1, tiled=True)  34.3 us
    gather x2, local copies, waits for them, and re-layouts, per_device(): looked_up = jnp.take(table, jnp.clip(ordered, 0, vocab_rows - 1), axis=0)  19.4 us
    all_gather x1, blocking collectives, per_device(): lax.all_gather(window_ids, 'batch', axis=1, tiled=True)  14.3 us
  transfers between devices with their start and end apart: 4, of which 3 were waited for; matrix products, arithmetic and copies ran while one was open for 4% of the time, Pallas kernels for 0%

profile of v1, /device:TPU:10, one launch (start us, length us, event | category | flops | bytes accessed | tf_op | source)
XLA Modules:
  0.0 405.5 jit_solution(11319681605078466096)
XLA Ops:
  7.2 0.8 copy.76
  8.1 14.3 %all_gather.6 = s32[3,16,8]{2,0,1:T(4,128)S(1)} all-gather(s32[3,2,8]{2,0,1:T(4,128)S(1)} %copy.76), channel_id=1, replica_groups=mesh['batch'=8,'vocab'=4] {'batch'}, dimensions={1}, use_global_device_ids=true | all-gather | bytes 1728 | tf_op jit(solution)/shard_map/all_gather | solution.py:75
  22.8 12.2 %gather_fusion = bf16[384,4608]{1,0:T(8,128)(2,1)} fusion(bf16[512,4608]{1,0:T(8,128)(2,1)} %param.20, s32[1024]{0:T(1024)S(1)} %pad_clamp_fusion), kind=kCustom, calls=%fused_computation | custom fusion | bytes 7079424 | tf_op jit(solution)/shard_map/jit(_take)/gather | solution.py:82
  35.0 7.3 %reshape.736 = bf16[16,8,3,4608]{3,2,1,0:T(4,128)(2,1)} reshape(bf16[384,4608]{1,0:T(8,128)(2,1)} %gather_fusion) | data formatting | bytes 7077888 | tf_op jit(solution)/shard_map/jit(_take)/gather | solution.py:82
  42.4 6.3 %select_convert_fusion = bf16[16,8,3,4608]{3,1,2,0:T(8,128)(2,1)} fusion(bf16[16,8,3,4608]{3,2,1,0:T(4,128)(2,1)} %reshape.736, pred[16,8,3]{1,2,0:T(4,128)(4,1)S(1)} %copy.79, pred[16,8,3]{1,2,0:T(4,128)(4,1)S(1)} %copy.78), kind=kLoop, calls=%fused_computation.1 | loop fusion | flops 7077888 | bytes 7078656 | tf_op jit(solution)/shard_map/convert_element_type | solution.py:85
  48.8 4.3 %copy.102 = bf16[256,4608]{1,0:T(8,128)(2,1)} copy(bf16[256,4608]{0,1:T(8,128)(2,1)} %bitcast.319) | data formatting | bytes 4718592 | tf_op jit(solution)/shard_map/dot_general | solution.py:108
  53.7 36.1 %reduce-scatter.2.cloned.1.call-done = bf16[2,8,3,4608]{3,1,2,0:T(8,128)(2,1)} async-done(((bf16[16,8,3,4608]{3,1,2,0:T(8,128)(2,1)}), bf16[2,8,3,4608]{3,1,2,0:T(8,128)(2,1)}) %reduce-scatter.2.cloned.1.call-update) | async-done | bytes 442384 | tf_op jit(solution)/shard_map/reduce_scatter | solution.py:84
  89.8 1.8 copy.82
  92.1 47.6 %all-reduce.13.cloned.1.call-done = bf16[2,8,3,4608]{3,1,0,2:T(8,128)(2,1)} async-done(((bf16[2,8,3,4608]{3,1,0,2:T(8,128)(2,1)}), bf16[2,8,3,4608]{3,1,0,2:T(8,128)(2,1)}) %all-reduce.13.cloned.1.call-update) | async-done | bytes 442384 | tf_op jit(solution)/shard_map/psum | solution.py:87
  139.7 1.2 convert_element_type.164
  141.1 1.6 fusion.45
  142.7 1.7 fusion.48
  147.1 0.7 fusion.89
  149.9 1.2 fusion.71
  151.1 1.2 fusion.70
  152.4 1.2 fusion.69
  153.6 50.6 %all-reduce.15.cloned.1.call-done = (f32[16,4608]{1,0:T(8,128)}, f32[16,4608]{1,0:T(8,128)}, f32[16,4608]{1,0:T(8,128)}) async-done(((f32[16,4608]{1,0:T(8,128)}, f32[16,4608]{1,0:T(8,128)}, f32[16,4608]{1,0:T(8,128)}), (f32[16,4608]{1,0:T(8,128)}, f32[16,4608]{1,0:T(8,128)}, f32[16,4608]{1,0:T(8,128)})) %all-reduce.15.cloned.1.call-update) | async-done | bytes 884752 | tf_op jit(solution)/shard_map/psum | solution.py:134
  204.2 1.2 multiply_reduce_fusion.1
  205.4 1.1 multiply_reduce_fusion.3
  206.5 1.1 multiply_reduce_fusion.5
  207.6 1.5 multiply_reduce_fusion.4
  209.6 32.6 %all_to_all.15 = bf16[8,16,4608]{2,1,0:T(8,128)(2,1)} all-to-all(bf16[8,16,4608]{2,1,0:T(8,128)(2,1)S(1)} %stack.12), channel_id=1, replica_groups=mesh['batch'=8,'vocab'=4] {'batch'}, dimensions={0} | all-to-all | bytes 2359296 | tf_op jit(solution)/shard_map/all_to_all | solution.py:140
  242.3 32.5 %all_to_all.16 = bf16[8,16,4608]{2,1,0:T(8,128)(2,1)} all-to-all(bf16[8,16,4608]{2,1,0:T(8,128)(2,1)S(1)} %stack.13), channel_id=1, replica_groups=mesh['batch'=8,'vocab'=4] {'batch'}, dimensions={0} | all-to-all | bytes 2359296 | tf_op jit(solution)/shard_map/all_to_all | solution.py:140
  274.8 1.1 stack.14
  275.9 5.9 %all-to-all-start.2 = ((bf16[8,16,4608]{2,1,0:T(8,128)(2,1)}), bf16[8,16,4608]{2,1,0:T(8,128)(2,1)}, u32[]{:S(2)}, u32[]{:S(2)}) async-start(bf16[8,16,4608]{2,1,0:T(8,128)(2,1)} %stack.14), calls=%async_computation.3 | async-start | bytes 2359296 | tf_op jit(solution)/shard_map/all_to_all | solution.py:140
  281.9 34.3 %all_gather.7 = s32[3,16,8]{2,0,1:T(4,128)S(1)} all-gather(s32[3,2,8]{2,0,1:T(4,128)S(1)} %copy.92), channel_id=1, replica_groups=mesh['batch'=8,'vocab'=4] {'batch'}, dimensions={1}, use_global_device_ids=true | all-gather | bytes 1728 | tf_op jit(solution)/shard_map/all_gather | solution.py:76
  317.8 4.6 %select_reduce_fusion.2 = (f32[128]{0:T(128)S(1)}, f32[128]{0:T(128)S(1)}, f32[128]{0:T(128)S(1)}) fusion(s32[128]{0:T(128)S(1)} %sub.79, bf16[128,4608]{1,0:T(8,128)(2,1)} %bitcast.318, bf16[512,4608]{1,0:T(8,128)(2,1)} %param.20), kind=kOutput, calls=%fused_computation.103 | convolution fusion | flops 604438144 | bytes 5900288 | tf_op jit(solution)/shard_map/dot_general | solution.py:138
  322.4 4.1 %select_reduce_fusion.1 = (f32[128]{0:T(128)S(1)}, f32[128]{0:T(128)S(1)}, f32[128]{0:T(128)S(1)}) fusion(s32[128]{0:T(128)S(1)} %sub.82, bf16[128,4608]{1,0:T(8,128)(2,1)S(1)} %bitcast.317, bf16[512,4608]{1,0:T(8,128)(2,1)} %param.20), kind=kOutput, calls=%fused_computation.101 | convolution fusion | flops 604438144 | bytes 5900288 | tf_op jit(solution)/shard_map/dot_general | solution.py:138
  326.5 4.5 %select_reduce_fusion = (f32[128]{0:T(128)S(1)}, f32[128]{0:T(128)S(1)}, f32[128]{0:T(128)S(1)}) fusion(s32[128]{0:T(128)S(1)} %sub.85, bf16[128,4608]{1,0:T(8,128)(2,1)} %bitcast.90, bf16[512,4608]{1,0:T(8,128)(2,1)} %param.20), kind=kOutput, calls=%fused_computation.99 | convolution fusion | flops 604438144 | bytes 5900288 | tf_op jit(solution)/shard_map/dot_general | solution.py:138
  331.0 13.3 %all-reduce.7 = (f32[128]{0:T(128)S(1)}, f32[128]{0:T(128)S(1)}, f32[128]{0:T(128)S(1)}, f32[128]{0:T(128)S(1)}, f32[128]{0:T(128)S(1)}, /*index=5*/f32[128]{0:T(128)S(1)}) all-reduce(f32[128]{0:T(128)S(1)} %get-tuple-element.17, f32[128]{0:T(128)S(1)} %get-tuple-element.14, ...), channel_id=5, replica_groups=mesh['batch'=8,'vocab'=4] {'batch'}, use_global_device_ids=true, to_apply=%region_24.25.clone | all-reduce | flops 768 | bytes 6144
  344.8 7.9 %all-reduce.8 = (f32[16]{0:T(128)S(1)}, f32[16]{0:T(128)S(1)}, f32[16]{0:T(128)S(1)}, f32[16]{0:T(128)S(1)}, f32[16]{0:T(128)S(1)}, /*index=5*/f32[16]{0:T(128)S(1)}) all-reduce(f32[16]{0:T(128)S(1)} %dynamic-slice.5, f32[16]{0:T(128)S(1)} %dynamic-slice.3, f32[16]{0:T(128)S(1)} %dynamic-slice.1, ...), channel_id=1, replica_groups=mesh['batch'=8,'vocab'=4] {'vocab'}, use_global_device_ids=true, to_apply=%region_25.26 | all-reduce | flops 96 | bytes 768 | tf_op jit(solution)/shard_map/psum | solution.py:158
  353.0 43.5 %all-reduce.6 = (f32[128]{0:T(128)S(1)}, f32[128]{0:T(128)S(1)}, f32[128]{0:T(128)S(1)}) all-reduce(f32[128]{0:T(128)S(1)} %get-tuple-element.16, f32[128]{0:T(128)S(1)} %get-tuple-element.13, f32[128]{0:T(128)S(1)} %get-tuple-element.10), channel_id=1, replica_groups=mesh['batch'=8,'vocab'=4] {'batch','vocab'}, use_global_device_ids=true, to_apply=%region_31.32 | all-reduce | flops 384 | bytes 3072 | tf_op jit(solution)/shard_map/pmax | solution.py:159
  (123 shorter events, 11.2 us)
Async XLA Ops:
  7.2 142.7 %copy-start = (bf16[256,4608]{1,0:T(8,128)(2,1)S(1)}, bf16[256,4608]{1,0:T(8,128)(2,1)}, u32[]{:S(2)}) copy-start(bf16[256,4608]{1,0:T(8,128)(2,1)} %param.27) | copy-start | bytes 7077892
  7.2 82.6 %reduce-scatter.2.cloned.1.call-start = ((), (), s32[]{:S(2)}) async-start(), calls=%async_computation.4 | async-start | bytes 3981312 | tf_op jit(solution)/shard_map/reduce_scatter | solution.py:84
  48.7 90.9 %all-reduce.13.cloned.1.call-start = ((), (), s32[]{:S(2)}) async-start(), calls=%async_computation.5 | async-start | bytes 884736 | tf_op jit(solution)/shard_map/psum | solution.py:87
  48.8 4.4 %copy-start.15 = (s32[2]{0:T(128)S(1)}, s32[2]{0:T(128)}, u32[]{:S(2)}) copy-start(s32[2]{0:T(128)} %param.19) | copy-start | bytes 28
  48.8 4.5 %copy-start.13 = (s32[2,2]{1,0:T(2,128)S(1)}, s32[2,2]{1,0:T(2,128)}, u32[]{:S(2)}) copy-start(s32[2,2]{1,0:T(2,128)} %param.17) | copy-start | bytes 52
  48.8 4.5 %copy-start.14 = (s32[2,2]{1,0:T(2,128)S(1)}, s32[2,2]{1,0:T(2,128)}, u32[]{:S(2)}) copy-start(s32[2,2]{1,0:T(2,128)} %param.18) | copy-start | bytes 52
  53.2 87.9 %copy-start.5 = (f32[4608]{0:T(1024)S(1)}, f32[4608]{0:T(1024)}, u32[]{:S(2)}) copy-start(f32[4608]{0:T(1024)} %param.21) | copy-start | bytes 55300
  91.6 112.6 %all-reduce.15.cloned.1.call-start = ((), (), s32[]{:S(2)}) async-start(), calls=%async_computation.6 | async-start | bytes 1769472 | tf_op jit(solution)/shard_map/psum | solution.py:134
  139.7 4.7 %copy-start.3 = (bf16[4608,128]{1,0:T(8,128)(2,1)S(1)}, bf16[4608,128]{1,0:T(8,128)(2,1)}, u32[]{:S(2)}) copy-start(bf16[4608,128]{1,0:T(8,128)(2,1)} %param.26) | copy-start | bytes 3538948
  142.6 2.4 copy-start.2
  144.7 1.7 copy-start.1
  147.1 1.7 copy-start.16
  147.8 2.1 copy-start.9
  152.4 55.3 %copy-start.10 = (f32[4608]{0:T(1024)S(1)}, f32[4608]{0:T(1024)}, u32[]{:S(2)}) copy-start(f32[4608]{0:T(1024)} %param.22) | copy-start | bytes 55300
  153.6 55.6 %copy-start.11 = (f32[4608]{0:T(1024)S(1)}, f32[4608]{0:T(1024)}, u32[]{:S(2)}) copy-start(f32[4608]{0:T(1024)} %param.23) | copy-start | bytes 55300
  204.2 5.0 %copy-start.6 = (f32[16,4608]{1,0:T(8,128)S(1)}, f32[16,4608]{1,0:T(8,128)}, u32[]{:S(2)}) copy-start(f32[16,4608]{1,0:T(8,128)} %get-tuple-element.36) | copy-start | bytes 884740
  204.2 5.0 %copy-start.7 = (f32[16,4608]{1,0:T(8,128)S(1)}, f32[16,4608]{1,0:T(8,128)}, u32[]{:S(2)}) copy-start(f32[16,4608]{1,0:T(8,128)} %get-tuple-element.37) | copy-start | bytes 884740
  204.2 5.0 %copy-start.8 = (f32[16,4608]{1,0:T(8,128)S(1)}, f32[16,4608]{1,0:T(8,128)}, u32[]{:S(2)}) copy-start(f32[16,4608]{1,0:T(8,128)} %get-tuple-element.38) | copy-start | bytes 884740
  274.8 7.1 %copy-start.12 = (s32[3,2,8]{2,1,0:T(2,128)S(1)}, s32[3,2,8]{2,1,0:T(2,128)}, u32[]{:S(2)}) copy-start(s32[3,2,8]{2,1,0:T(2,128)} %param.16) | copy-start | bytes 580
  274.8 41.7 %copy-start.17 = (u32[32]{0:T(128)S(1)}, u32[32]{0:T(128)}, u32[]{:S(2)}) copy-start(u32[32]{0:T(128)} %constant.94) | copy-start | bytes 388
  275.9 50.6 %all-to-all-start.2 = ((bf16[8,16,4608]{2,1,0:T(8,128)(2,1)}), bf16[8,16,4608]{2,1,0:T(8,128)(2,1)}, u32[]{:S(2)}, u32[]{:S(2)}) async-start(bf16[8,16,4608]{2,1,0:T(8,128)(2,1)} %stack.14), calls=%async_computation.3 | async-start | bytes 2359296 | tf_op jit(solution)/shard_map/all_to_all | solution.py:140
  317.8 4.6 %copy-start.4 = (bf16[8,16,4608]{2,1,0:T(8,128)(2,1)S(1)}, bf16[8,16,4608]{2,1,0:T(8,128)(2,1)}, u32[]{:S(2)}) copy-start(bf16[8,16,4608]{2,1,0:T(8,128)(2,1)} %all_to_all.16) | copy-start | bytes 3538948
Sparse Core Ops, SparseCore 0:
  48.9 40.8 reduce-scatter.1
  92.8 46.8 all-reduce.12
  153.7 50.3 all-reduce.14
